TPU v7x, 128 devices: a whole 4x4x4 slice. The times are simulated.
128 devices in a mesh: gx: 8 (over z, core), wa: 16 (over x, y).
Axes of the slice: x: 4, y: 4, z: 4, core: 2. Of those that a mesh axis runs over, the one named last changes fastest.
Arguments:
- positions: float32 [2048, 3, 256], P(('gx', 'wa')), may hold values from 0 to 1
- weights: float32 [2048, 256], P(('gx', 'wa')), may hold values from 0.5 to 2
- block_count: int32 [2048], P(('gx', 'wa')), may hold values from 1 to 256
- send_list: int32 [128, 16, 2], P(('gx', 'wa')), may hold values from 0 to 15
- unit_pair: int32 [128, 32], P(('gx', 'wa')), may hold values from 0 to 31, each once within a row
- unit_live: int32 [128], P(('gx', 'wa')), may hold values from 4 to 32, as said below
Outputs:
- slab_counts: float32 [8, 30, 20], P('gx')
- totals: float32 [30, 20], replicated
Inputs may be any that keep to these rules, and one draw needn't show every extreme that they name: `unit_pair`: each row holds every slot number once. `unit_live`: the active units of a device are the first ones of its list; some device has all 32 active.
All inputs are finite; a program needn't handle non-finite values.
Results may differ from a plain program's by a relative error of at most 0.0003.
Values sent between devices are 32-bit elements; how exact they have to be, the bound alone decides.
A program may use at most 64 MiB of HBM per device.

v0:
```python
import functools

import jax
import jax.numpy as jnp
from jax import lax
from jax.experimental import pallas as pl
from jax.experimental.pallas import tpu as pltpu
from jax.sharding import PartitionSpec as P

SBINS = 30
MUBINS = 20
HS, HM = SBINS // 2, MUBINS // 2
reach = 0.5
viewer = (0.5, 0.5, -1.5)
TILES = 32
f32, bf16, i32 = jnp.float32, jnp.bfloat16, jnp.int32
MESH = pl.DeviceIdType.MESH


def hats(at, first, second, half):
    spot = jnp.concatenate([at, at - half], axis=0).astype(bf16)
    first = jnp.concatenate([first, first], axis=0).astype(bf16)
    second = jnp.concatenate([second, second], axis=0).astype(bf16)
    zero = jnp.zeros_like(first)
    before = spot == jnp.asarray(-1, bf16)
    out = []
    for q in range(half):
        here = spot == jnp.asarray(q, bf16)
        out.append(jnp.where(here, first, jnp.where(before, second, zero)))
        before = here
    return out


def tile_hats(cols, lane_at, row):
    def of_a(c):
        return jnp.take_along_axis(cols, jnp.full((8, 128), lane_at + c, i32), axis=1)

    def of_b(c):
        return jnp.broadcast_to(row[c : c + 1, :], (8, 128))

    dx, dy, dz = (of_a(c) - of_b(c) for c in range(3))
    square = dx * dx + dy * dy + dz * dz
    norm_a, norm_b = of_a(3), of_b(3)
    s = square * lax.rsqrt(jnp.maximum(square, 1e-30)) - 0.5
    s_at = jnp.floor(s)
    s_part = s - s_at
    mu = (MUBINS / 2) * jnp.abs(norm_a - norm_b) * lax.rsqrt(
        jnp.maximum(square, 1.0) * (norm_a + norm_b - square)
    ) - 0.5
    mu_at = jnp.floor(mu)
    both = of_a(4) * of_b(4)
    upper = (mu - mu_at) * both
    return hats(s_at, 1.0 - s_part, s_part, HS), hats(mu_at, both - upper, upper, HM)


def iota(shape, d):
    return lax.broadcasted_iota(i32, shape, d)


def plan(a_weights, b_weights):
    def live(halves):
        count = sum(jnp.where(w > 0.0, 1.0, 0.0) for w in halves)
        return jnp.broadcast_to(jnp.sum(count, axis=1, keepdims=True), count.shape)

    n_a, n_b = live(a_weights), live(b_weights)
    rows_a, rows_b = jnp.ceil(n_a / 8), jnp.ceil(n_b / 8)
    lanes_a, lanes_b = jnp.ceil(n_a / 128), jnp.ceil(n_b / 128)
    turned = jnp.where(rows_b * lanes_a < rows_a * lanes_b, 1.0, 0.0)
    n_lanes = jnp.where(turned > 0.0, lanes_a, lanes_b)
    return turned, n_lanes, jnp.where(turned > 0.0, rows_b, rows_a) * n_lanes


def slot_copy(src, dst, send_sem, recv_sem, device):
    return pltpu.make_async_remote_copy(
        src_ref=src, dst_ref=dst, send_sem=send_sem, recv_sem=recv_sem, device_id=device, device_id_type=MESH
    )


def exchange_kernel(
    n_gx, n_wa, count_ref, list_ref, pair_ref, live_ref, pos_ref, wgt_ref, out_ref,
    home_ref, stage_ref, own_ref, below_ref, partner_ref, deal_ref, send_sems, own_sems, below_sems, deal_sems,
):
    g, w = lax.axis_index("gx"), lax.axis_index("wa")
    above, under = lax.rem(g + 1, n_gx), lax.rem(g + n_gx - 1, n_gx)
    units = 2 * n_wa
    barrier = pltpu.get_barrier_semaphore()

    def greet(o, carry):
        p = lax.rem(w + o, n_wa)
        pl.semaphore_signal(barrier, inc=1, device_id=(under, p), device_id_type=MESH)

        @pl.when(o > 0)
        def _():
            pl.semaphore_signal(barrier, inc=1, device_id=(g, p), device_id_type=MESH)

        return carry

    lax.fori_loop(0, n_wa, greet, 0)

    for b in range(pos_ref.shape[0]):
        for h in range(2):
            at = slice(128 * h, 128 * (h + 1))
            home_ref[b, 4 * h : 4 * h + 3, :] = pos_ref[b, :, at]
            keep = iota((1, 128), 1) + 128 * h < count_ref[b]
            home_ref[b, 4 * h + 3 : 4 * h + 4, :] = jnp.where(keep, wgt_ref[b : b + 1, at], 0.0)
    for q in range(units):
        stage_ref[q] = home_ref[list_ref[0, q // 2, q % 2]]
    pl.semaphore_wait(barrier, 2 * n_wa - 1)

    def own_copy(p, rank):
        return slot_copy(
            stage_ref.at[pl.ds(2 * p, 2)], own_ref.at[pl.ds(2 * rank, 2)], send_sems.at[0, p], own_sems.at[rank], (g, p)
        )

    def below_copy(p, rank):
        return slot_copy(
            stage_ref.at[pl.ds(2 * p, 2)], below_ref.at[pl.ds(2 * rank, 2)], send_sems.at[1, p], below_sems.at[rank], (above, p)
        )

    def send(o, carry):
        p = lax.rem(w + o, n_wa)
        below_copy(p, w).start()

        @pl.when(o > 0)
        def _():
            own_copy(p, w).start()

        return carry

    lax.fori_loop(0, n_wa, send, 0)
    own_ref[pl.ds(2 * w, 2)] = stage_ref[pl.ds(2 * w, 2)]

    def arrive(o, carry):
        p = lax.rem(w + o, n_wa)
        below_copy(p, p).wait_recv()

        @pl.when(o > 0)
        def _():
            own_copy(p, p).wait_recv()

        return carry

    lax.fori_loop(0, n_wa, arrive, 0)
    for u in range(units):
        partner_ref[u] = below_ref[pair_ref[0, u]]

    active = iota((units, 128), 0) < live_ref[0]
    a_rows = [own_ref[:, c, :] for c in range(8)]
    b_rows = [partner_ref[:, c, :] for c in range(8)]
    for c in (3, 7):
        a_rows[c] = jnp.where(active, a_rows[c], 0.0)
    tiles = plan((a_rows[3], a_rows[7]), (b_rows[3], b_rows[7]))[2]
    unit = iota((units, 128), 0).astype(f32)
    key = tiles * units + (units - 1 - unit)
    on_lanes = jnp.sum(jnp.where(iota((units, 128), 0) == iota((units, 128), 1), key, 0.0), axis=0, keepdims=True)
    more = (on_lanes > key) & (iota((units, 128), 1) < units)
    rank = jnp.sum(jnp.where(more, 1.0, 0.0), axis=1, keepdims=True)
    place = jnp.where(rank < n_wa, rank, (units - 1 + n_wa) - rank)
    place = jnp.sum(
        jnp.where(iota((units, units), 0) == iota((units, units), 1), place, 0.0), axis=0, keepdims=True
    )
    choice = jnp.where(iota((units, units), 0).astype(f32) == place, 1.0, 0.0)
    chosen = jnp.dot(
        choice, jnp.concatenate(a_rows + b_rows, axis=1), precision=lax.Precision.HIGHEST, preferred_element_type=f32
    )
    for t in range(2):
        for s in range(2):
            for c in range(8):
                at = (8 * s + c) * 128
                deal_ref[:, 2 * t + s, c, :] = chosen[t * n_wa : (t + 1) * n_wa, at : at + 128]

    def deal_copy(o, p, rank):
        return slot_copy(deal_ref.at[o], out_ref.at[rank], send_sems.at[2, o], deal_sems.at[rank], (g, p))

    def deal(o, carry):
        deal_copy(o, lax.rem(w + o, n_wa), w).start()
        return carry

    lax.fori_loop(1, n_wa, deal, 0)
    out_ref[w] = deal_ref[0]

    def finish(o, carry):
        p = lax.rem(w + o, n_wa)
        deal_copy(o, p, p).wait_recv()
        deal_copy(o, p, p).wait_send()
        own_copy(p, p).wait_send()
        below_copy(p, p).wait_send()
        return carry

    lax.fori_loop(1, n_wa, finish, 0)
    below_copy(w, w).wait_send()


def dealt_blocks(n_gx, n_wa, positions, weights, block_count, send_list, unit_pair, unit_live):
    smem, vmem = pl.BlockSpec(memory_space=pltpu.SMEM), pl.BlockSpec(memory_space=pltpu.VMEM)
    units = 2 * n_wa
    return pl.pallas_call(
        functools.partial(exchange_kernel, n_gx, n_wa),
        out_shape=jax.ShapeDtypeStruct((n_wa, 4, 8, 128), f32),
        in_specs=[smem] * 4 + [vmem] * 2,
        out_specs=vmem,
        scratch_shapes=[
            pltpu.VMEM((positions.shape[0], 8, 128), f32),
            pltpu.VMEM((units, 8, 128), f32),
            pltpu.VMEM((units, 8, 128), f32),
            pltpu.VMEM((units, 8, 128), f32),
            pltpu.VMEM((units, 8, 128), f32),
            pltpu.VMEM((n_wa, 4, 8, 128), f32),
            pltpu.SemaphoreType.DMA((3, n_wa)),
            pltpu.SemaphoreType.DMA((n_wa,)),
            pltpu.SemaphoreType.DMA((n_wa,)),
            pltpu.SemaphoreType.DMA((n_wa,)),
        ],
        compiler_params=pltpu.CompilerParams(collective_id=0, has_side_effects=True),
    )(block_count, send_list, unit_pair, unit_live, positions, weights)


def total_kernel(n_gx, n_wa, scale, in_ref, slab_out, whole_out, wa_ref, gx_ref, slab_ref, send_sems, wa_sems, gx_sems):
    g, w = lax.axis_index("gx"), lax.axis_index("wa")
    barrier = pltpu.get_barrier_semaphore()

    def each(n, me, act):
        def step(o, carry):
            act(lax.rem(me + o, n))
            return carry

        lax.fori_loop(1, n, step, 0)

    each(n_wa, w, lambda p: pl.semaphore_signal(barrier, inc=1, device_id=(g, p), device_id_type=MESH))
    each(n_gx, g, lambda p: pl.semaphore_signal(barrier, inc=1, device_id=(p, w), device_id_type=MESH))
    pl.semaphore_wait(barrier, n_wa + n_gx - 2)

    def wa_copy(p, rank):
        return slot_copy(in_ref, wa_ref.at[rank], send_sems.at[0, p], wa_sems.at[rank], (g, p))

    def gx_copy(p, rank):
        return slot_copy(slab_ref, gx_ref.at[rank], send_sems.at[1, p], gx_sems.at[rank], (p, w))

    each(n_wa, w, lambda p: wa_copy(p, w).start())
    wa_ref[w] = in_ref[...]
    each(n_wa, w, lambda p: wa_copy(p, p).wait_recv())
    slab = jnp.sum(wa_ref[...], axis=0) * scale
    slab_ref[...] = slab
    gx_ref[g] = slab

    def unpack(packed, out):
        for k in range(4):
            rows = min(8, SBINS - 8 * k)
            turned = packed if k == 0 else pltpu.roll(packed, 128 - 32 * k, 1)
            out[8 * k : 8 * k + rows, :] = turned[:rows, :MUBINS]

    each(n_gx, g, lambda p: gx_copy(p, g).start())
    unpack(slab, slab_out.at[0])
    each(n_wa, w, lambda p: wa_copy(p, p).wait_send())
    each(n_gx, g, lambda p: gx_copy(p, p).wait_recv())
    unpack(jnp.sum(gx_ref[...], axis=0) / n_gx, whole_out)
    each(n_gx, g, lambda p: gx_copy(p, p).wait_send())


def totals(n_gx, n_wa, scale, packed):
    vmem = pl.BlockSpec(memory_space=pltpu.VMEM)
    return pl.pallas_call(
        functools.partial(total_kernel, n_gx, n_wa, scale),
        out_shape=(
            jax.ShapeDtypeStruct((1, SBINS, MUBINS), f32),
            jax.ShapeDtypeStruct((SBINS, MUBINS), f32),
        ),
        in_specs=[vmem],
        out_specs=(vmem, vmem),
        scratch_shapes=[
            pltpu.VMEM((n_wa, 8, 128), f32),
            pltpu.VMEM((n_gx, 8, 128), f32),
            pltpu.VMEM((8, 128), f32),
            pltpu.SemaphoreType.DMA((2, n_wa)),
            pltpu.SemaphoreType.DMA((n_wa,)),
            pltpu.SemaphoreType.DMA((n_gx,)),
        ],
        compiler_params=pltpu.CompilerParams(collective_id=1, has_side_effects=True),
    )(packed)


def count_kernel(units, blocks_ref, out_ref, rows_ref, cols_ref, list_ref, list_smem, acc_ref, sem):
    n_blocks = 2 * units
    scale = SBINS / reach
    groups = n_blocks // 16
    for h in range(2):
        x, y, z, w = (blocks_ref[:, 4 * h + c, :] for c in range(4))
        norm = 0.0
        for c, v in enumerate((x, y, z)):
            rows_ref[pl.ds(h * n_blocks, n_blocks), c, :] = v * scale
            moved = (v + viewer[c]) * scale
            norm = norm + moved * moved
        rows_ref[pl.ds(h * n_blocks, n_blocks), 3, :] = 2.0 * norm
        rows_ref[pl.ds(h * n_blocks, n_blocks), 4, :] = w
        for c in range(5, 8):
            rows_ref[pl.ds(h * n_blocks, n_blocks), c, :] = jnp.zeros_like(w)
    far = 2.0 * sum((v * scale) ** 2 for v in viewer)
    rows_ref[2 * n_blocks] = jnp.where(
        lax.broadcasted_iota(i32, (8, 128), 0) == 3, jnp.float32(far), jnp.float32(0.0)
    )
    for k in range(2 * groups):
        cols_ref[k * 128 : (k + 1) * 128, :] = rows_ref[pl.ds(k * 16, 16)].reshape(128, 128).T

    def weights_of(s):
        return [blocks_ref[pl.ds(s, units, stride=2), 4 * h + 3, :] for h in range(2)]

    turned, n_lanes, tiles = plan(weights_of(0), weights_of(1))
    low = lax.broadcasted_iota(i32, (units, units), 1) < lax.broadcasted_iota(i32, (units, units), 0)
    start = jnp.dot(jnp.where(low, 1.0, 0.0), tiles, preferred_element_type=f32)
    total = jnp.sum(tiles, axis=0, keepdims=True)
    unit = lax.broadcasted_iota(i32, (units, 128), 0).astype(f32)
    pair8 = jnp.floor(unit / 8)
    lane16 = 2.0 * (unit - 8.0 * pair8) + turned
    row_const = pair8 * 16.0
    lane = lax.broadcasted_iota(i32, (units, 128), 1).astype(f32)
    n_list = list_ref.shape[0]
    dummy = jnp.float32(2 * n_blocks)
    list_ref[0] = jnp.broadcast_to(total, (8, 128)).astype(i32)

    def fill(k, carry):
        at = lane + k.astype(f32) * 128.0 - start
        inside = (at >= 0.0) & (at < tiles)
        row = jnp.where(n_lanes > 1.5, jnp.floor(at * 0.5), at)
        part = at - row * n_lanes
        half = jnp.floor(row / 16)
        row_at = half * (16.0 * groups) + row_const + (row - 16.0 * half)
        lane_row = part * n_blocks + 2.0 * unit + (1.0 - turned)
        code = row_at * 4096.0 + lane16 * 256.0 + lane_row
        value = jnp.sum(jnp.where(inside, code - dummy, 0.0), axis=0, keepdims=True) + dummy
        list_ref[k + 1] = jnp.broadcast_to(value, (8, 128)).astype(i32)
        return carry

    lax.fori_loop(0, n_list - 1, fill, 0)
    copy = pltpu.make_async_copy(list_ref.at[:, 0, :], list_smem, sem)
    copy.start()
    acc_ref[...] = jnp.zeros_like(acc_ref)
    copy.wait()
    trips = (list_smem[0, 0] + TILES - 1) // TILES

    def load(trip, t):
        place = trip * TILES + t
        code = list_smem[1 + (place >> 7), place & 127]
        at = pl.multiple_of((code >> 12) * 8, 8)
        return tile_hats(cols_ref[pl.ds(at, 8), :], ((code >> 8) & 15) * 8, rows_ref[code & 255])

    def body(trip, carry):
        total = None
        for p in range(TILES // 2):
            s0, m0 = load(trip, 2 * p)
            s1, m1 = load(trip, 2 * p + 1)
            s = jnp.concatenate([jnp.concatenate(s0, 0), jnp.concatenate(s1, 0)], 1)
            m = jnp.concatenate([jnp.concatenate(m0, 0), jnp.concatenate(m1, 0)], 1)
            r = lax.dot_general(s, m, (((1,), (1,)), ((), ())), preferred_element_type=f32)
            total = r if total is None else total + r
        acc_ref[...] += total
        return carry

    lax.fori_loop(0, trips, body, 0)

    sm = (16 * HS, 16 * HM)
    kept = jnp.where((iota(sm, 0) & 7) == (iota(sm, 1) & 7), acc_ref[...], 0.0)
    r, c = iota((32, 16 * HS), 0), iota((32, 16 * HS), 1)
    to_s = jnp.where((c >> 4) + HS * ((c >> 3) & 1) == r, 1.0, 0.0)
    r, c = iota((16 * HM, 128), 0), iota((16 * HM, 128), 1)
    to_m = jnp.where((r >> 4) + HM * ((r >> 3) & 1) == c, 1.0, 0.0)
    high = lax.Precision.HIGHEST
    by_s = jnp.dot(to_s, kept, precision=high, preferred_element_type=f32)
    bins = jnp.dot(by_s, to_m, precision=high, preferred_element_type=f32)
    packed = bins[0:8]
    for k in range(1, 4):
        packed = packed + pltpu.roll(bins[8 * k : 8 * k + 8], 32 * k, 1)
    out_ref[...] = packed


def pair_counts(blocks):
    units = blocks.shape[0] // 2
    n_list = 1 + (units * 64 + TILES + 127) // 128
    return pl.pallas_call(
        functools.partial(count_kernel, units),
        out_shape=jax.ShapeDtypeStruct((8, 128), f32),
        in_specs=[pl.BlockSpec(memory_space=pltpu.VMEM)],
        out_specs=pl.BlockSpec(memory_space=pltpu.VMEM),
        scratch_shapes=[
            pltpu.VMEM((4 * units + 1, 8, 128), f32),
            pltpu.VMEM((2 * (units // 8) * 128, 128), f32),
            pltpu.VMEM((n_list, 8, 128), i32),
            pltpu.SMEM((n_list, 128), i32),
            pltpu.VMEM((16 * HS, 16 * HM), f32),
            pltpu.SemaphoreType.DMA,
        ],
    )(blocks)


def solution(mesh):
    n_gx, n_wa = mesh.shape["gx"], mesh.shape["wa"]
    units = 2 * n_wa
    scale = 10.0 * SBINS * MUBINS / (n_wa * units * 256 * 256)

    def per_device(positions, weights, block_count, send_list, unit_pair, unit_live):
        dealt = dealt_blocks(n_gx, n_wa, positions, weights, block_count, send_list, unit_pair, unit_live)
        packed = pair_counts(dealt.reshape(2 * units, 8, 128))
        return totals(n_gx, n_wa, scale, packed)

    return jax.shard_map(
        per_device,
        mesh=mesh,
        in_specs=(P(("gx", "wa")),) * 6,
        out_specs=(P("gx", None, None), P()),
        check_vma=False,
    )
```

profile of v0, /device:TPU:1, one launch (start us, length us, event | category | flops | bytes accessed | tf_op | source)
XLA Modules:
  0.0 56.8 jit_solution(8670228958655998116)
XLA Ops:
  0.6 0.0 copy-start.1
  1.3 0.0 copy-done.1
  1.3 0.7 %copy.8.list_ref = s32[1,16,2]{2,1,0:T(8,128)} copy(s32[1,16,2]{1,2,0:T(2,128)S(1)} %copy-done.1) | data formatting | bytes 256 | tf_op args[3]
  2.0 1.5 %copy.9.pos_ref = f32[16,3,256]{2,1,0:T(4,128)} copy(f32[16,3,256]{2,0,1:T(8,128)} %param.6) | data formatting | bytes 98304 | tf_op args[0]
  3.5 22.0 %shard_map.77 = f32[16,4,8,128]{3,2,1,0:T(8,128)} custom-call(s32[16]{0:T(128)} %count_ref.1, s32[1,16,2]{2,1,0:T(8,128)} %copy.8.list_ref, s32[1,32]{1,0:T(1,128)} %pair_ref.1, s32[1]{0:T(128)S(6)} %copy.12.live_ref, f32[16,3,256]{2,1,0:T(4,128)} %copy.9.pos_ref, f32[16,256]{1,0:T(8,128)} %wgt_ref.1), custom_call_target="tpu_custom_call" | custom-call | tf_op jit(solution)/shard_map/pallas_call | solution.py:197
  25.4 11.7 %shard_map.78.in_ref = f32[8,128]{1,0:T(8,128)} custom-call(f32[64,8,128]{2,1,0:T(8,128)} %bitcast.1), custom_call_target="tpu_custom_call" | custom-call | tf_op jit(solution)/shard_map/pallas_call | solution.py:378
  37.2 17.6 %shard_map.79 = (f32[1,30,20]{2,1,0:T(8,128)}, f32[30,20]{1,0:T(8,128)}) custom-call(f32[8,128]{1,0:T(8,128)} %shard_map.78.in_ref), custom_call_target="tpu_custom_call" | custom-call | tf_op jit(solution)/shard_map/pallas_call | solution.py:262
  54.7 0.0 copy-start
  54.7 1.4 %copy.10 = f32[1,30,20]{1,0,2:T(1,128)} copy(f32[1,30,20]{2,1,0:T(8,128)} %get-tuple-element.2) | data formatting | bytes 4800 | tf_op jit(solution)/shard_map/pallas_call | solution.py:262
  56.1 0.0 copy-done
  56.1 0.7 %copy.11 = f32[30,20]{0,1:T(8,128)} copy(f32[30,20]{1,0:T(8,128)S(1)} %copy-done) | data formatting | bytes 4800 | tf_op jit(solution)/shard_map/pallas_call | solution.py:262
Async XLA Ops:
  0.6 0.7 %copy-start.1 = (s32[1,16,2]{1,2,0:T(2,128)S(1)}, s32[1,16,2]{1,2,0:T(2,128)}, u32[]{:S(2)}) copy-start(s32[1,16,2]{1,2,0:T(2,128)} %param.9) | copy-start | bytes 388
  54.7 1.4 %copy-start = (f32[30,20]{1,0:T(8,128)S(1)}, f32[30,20]{1,0:T(8,128)}, u32[]{:S(2)}) copy-start(f32[30,20]{1,0:T(8,128)} %get-tuple-element.3) | copy-start | bytes 7204
where the time goes:
time: 57.5 us; the launch traced here: 56.8 us
  Pallas kernels  51.2 us (89%)
  local copies, waits for them, and re-layouts  4.25 us (7%)
  between operations  1.33 us (2%)
    pallas_call x1, Pallas kernels, dealt_blocks(): pl.pallas_call(functools.partial(exchange_kernel, n_gx, n_wa), out_shape=...  22 us
    pallas_call x1, Pallas kernels, totals(): pl.pallas_call(functools.partial(total_kernel, n_gx, n_wa, scale), out_sh...  17.6 us
    pallas_call x1, Pallas kernels, pair_counts(): pl.pallas_call(functools.partial(count_kernel, units), out_shape=jax.Shap...  11.7 us
    unnamed x6, local copies, waits for them, and re-layouts  2.16 us
    pallas_call x2, local copies, waits for them, and re-layouts, totals(): pl.pallas_call(functools.partial(total_kernel, n_gx, n_wa, scale), out_sh...  2.08 us

commit v1 on v0

--- a/solution.py
+++ b/solution.py
@@ -31,9 +31,16 @@
     return out
 
 
+def lane_pick(x, lane):
+    numbers = lax.GatherDimensionNumbers(
+        offset_dims=(), collapsed_slice_dims=(1,), start_index_map=(1,), operand_batching_dims=(0,), start_indices_batching_dims=(0,)
+    )
+    return lax.gather(x, lane[..., None], numbers, slice_sizes=(1, 1), mode=lax.GatherScatterMode.PROMISE_IN_BOUNDS)
+
+
 def tile_hats(cols, lane_at, row):
     def of_a(c):
-        return jnp.take_along_axis(cols, jnp.full((8, 128), lane_at + c, i32), axis=1)
+        return lane_pick(cols, jnp.full((8, 128), lane_at + c, i32))
 
     def of_b(c):
         return jnp.broadcast_to(row[c : c + 1, :], (8, 128))
@@ -97,14 +104,14 @@
 
     lax.fori_loop(0, n_wa, greet, 0)
 
-    for b in range(pos_ref.shape[0]):
+    for b in range(pos_ref.shape[1]):
         for h in range(2):
             at = slice(128 * h, 128 * (h + 1))
-            home_ref[b, 4 * h : 4 * h + 3, :] = pos_ref[b, :, at]
+            home_ref[b, 4 * h : 4 * h + 3, :] = pos_ref[:, b, at]
             keep = iota((1, 128), 1) + 128 * h < count_ref[b]
             home_ref[b, 4 * h + 3 : 4 * h + 4, :] = jnp.where(keep, wgt_ref[b : b + 1, at], 0.0)
     for q in range(units):
-        stage_ref[q] = home_ref[list_ref[0, q // 2, q % 2]]
+        stage_ref[q] = home_ref[list_ref[0, q % 2, q // 2]]
     pl.semaphore_wait(barrier, 2 * n_wa - 1)
 
     def own_copy(p, rank):
@@ -170,14 +177,14 @@
                 deal_ref[:, 2 * t + s, c, :] = chosen[t * n_wa : (t + 1) * n_wa, at : at + 128]
 
     def deal_copy(o, p, rank):
-        return slot_copy(deal_ref.at[o], out_ref.at[rank], send_sems.at[2, o], deal_sems.at[rank], (g, p))
+        return slot_copy(deal_ref.at[o], out_ref.at[pl.ds(4 * rank, 4)], send_sems.at[2, o], deal_sems.at[rank], (g, p))
 
     def deal(o, carry):
         deal_copy(o, lax.rem(w + o, n_wa), w).start()
         return carry
 
     lax.fori_loop(1, n_wa, deal, 0)
-    out_ref[w] = deal_ref[0]
+    out_ref[pl.ds(4 * w, 4)] = deal_ref[0]
 
     def finish(o, carry):
         p = lax.rem(w + o, n_wa)
@@ -196,11 +203,11 @@
     units = 2 * n_wa
     return pl.pallas_call(
         functools.partial(exchange_kernel, n_gx, n_wa),
-        out_shape=jax.ShapeDtypeStruct((n_wa, 4, 8, 128), f32),
+        out_shape=pltpu.VMEM((2 * units, 8, 128), f32),
         in_specs=[smem] * 4 + [vmem] * 2,
         out_specs=vmem,
         scratch_shapes=[
-            pltpu.VMEM((positions.shape[0], 8, 128), f32),
+            pltpu.VMEM((positions.shape[1], 8, 128), f32),
             pltpu.VMEM((units, 8, 128), f32),
             pltpu.VMEM((units, 8, 128), f32),
             pltpu.VMEM((units, 8, 128), f32),
@@ -215,7 +222,7 @@
     )(block_count, send_list, unit_pair, unit_live, positions, weights)
 
 
-def total_kernel(n_gx, n_wa, scale, in_ref, slab_out, whole_out, wa_ref, gx_ref, slab_ref, send_sems, wa_sems, gx_sems):
+def total_kernel(n_gx, n_wa, in_ref, slab_out, whole_out, wa_ref, gx_ref, slab_ref, send_sems, wa_sems, gx_sems):
     g, w = lax.axis_index("gx"), lax.axis_index("wa")
     barrier = pltpu.get_barrier_semaphore()
 
@@ -239,31 +246,31 @@
     each(n_wa, w, lambda p: wa_copy(p, w).start())
     wa_ref[w] = in_ref[...]
     each(n_wa, w, lambda p: wa_copy(p, p).wait_recv())
-    slab = jnp.sum(wa_ref[...], axis=0) * scale
+    slab = jnp.sum(wa_ref[...], axis=0)
     slab_ref[...] = slab
     gx_ref[g] = slab
 
     def unpack(packed, out):
-        for k in range(4):
-            rows = min(8, SBINS - 8 * k)
+        for k in range(3):
+            rows = min(8, MUBINS - 8 * k)
             turned = packed if k == 0 else pltpu.roll(packed, 128 - 32 * k, 1)
-            out[8 * k : 8 * k + rows, :] = turned[:rows, :MUBINS]
+            out[8 * k : 8 * k + rows, :] = turned[:rows, :SBINS]
 
     each(n_gx, g, lambda p: gx_copy(p, g).start())
-    unpack(slab, slab_out.at[0])
+    unpack(slab, slab_out.at[:, 0, :])
     each(n_wa, w, lambda p: wa_copy(p, p).wait_send())
     each(n_gx, g, lambda p: gx_copy(p, p).wait_recv())
-    unpack(jnp.sum(gx_ref[...], axis=0) / n_gx, whole_out)
+    unpack(jnp.sum(gx_ref[...], axis=0), whole_out)
     each(n_gx, g, lambda p: gx_copy(p, p).wait_send())
 
 
-def totals(n_gx, n_wa, scale, packed):
+def totals(n_gx, n_wa, packed):
     vmem = pl.BlockSpec(memory_space=pltpu.VMEM)
     return pl.pallas_call(
-        functools.partial(total_kernel, n_gx, n_wa, scale),
+        functools.partial(total_kernel, n_gx, n_wa),
         out_shape=(
-            jax.ShapeDtypeStruct((1, SBINS, MUBINS), f32),
-            jax.ShapeDtypeStruct((SBINS, MUBINS), f32),
+            pltpu.VMEM((MUBINS, 1, SBINS), f32),
+            pltpu.VMEM((MUBINS, SBINS), f32),
         ),
         in_specs=[vmem],
         out_specs=(vmem, vmem),
@@ -359,15 +366,15 @@
 
     sm = (16 * HS, 16 * HM)
     kept = jnp.where((iota(sm, 0) & 7) == (iota(sm, 1) & 7), acc_ref[...], 0.0)
-    r, c = iota((32, 16 * HS), 0), iota((32, 16 * HS), 1)
-    to_s = jnp.where((c >> 4) + HS * ((c >> 3) & 1) == r, 1.0, 0.0)
-    r, c = iota((16 * HM, 128), 0), iota((16 * HM, 128), 1)
-    to_m = jnp.where((r >> 4) + HM * ((r >> 3) & 1) == c, 1.0, 0.0)
+    r, c = iota((32, 16 * HM), 0), iota((32, 16 * HM), 1)
+    to_m = jnp.where((c >> 4) + HM * ((c >> 3) & 1) == r, 1.0, 0.0)
+    r, c = iota((16 * HS, 128), 0), iota((16 * HS, 128), 1)
+    to_s = jnp.where((r >> 4) + HS * ((r >> 3) & 1) == c, 1.0, 0.0)
     high = lax.Precision.HIGHEST
-    by_s = jnp.dot(to_s, kept, precision=high, preferred_element_type=f32)
-    bins = jnp.dot(by_s, to_m, precision=high, preferred_element_type=f32)
+    by_m = lax.dot_general(to_m, kept, (((1,), (1,)), ((), ())), precision=high, preferred_element_type=f32)
+    bins = jnp.dot(by_m, to_s, precision=high, preferred_element_type=f32)
     packed = bins[0:8]
-    for k in range(1, 4):
+    for k in range(1, 3):
         packed = packed + pltpu.roll(bins[8 * k : 8 * k + 8], 32 * k, 1)
     out_ref[...] = packed
 
@@ -377,7 +384,7 @@
     n_list = 1 + (units * 64 + TILES + 127) // 128
     return pl.pallas_call(
         functools.partial(count_kernel, units),
-        out_shape=jax.ShapeDtypeStruct((8, 128), f32),
+        out_shape=pltpu.VMEM((8, 128), f32),
         in_specs=[pl.BlockSpec(memory_space=pltpu.VMEM)],
         out_specs=pl.BlockSpec(memory_space=pltpu.VMEM),
         scratch_shapes=[
@@ -397,9 +404,13 @@
     scale = 10.0 * SBINS * MUBINS / (n_wa * units * 256 * 256)
 
     def per_device(positions, weights, block_count, send_list, unit_pair, unit_live):
-        dealt = dealt_blocks(n_gx, n_wa, positions, weights, block_count, send_list, unit_pair, unit_live)
-        packed = pair_counts(dealt.reshape(2 * units, 8, 128))
-        return totals(n_gx, n_wa, scale, packed)
+        dealt = dealt_blocks(
+            n_gx, n_wa, jnp.transpose(positions, (1, 0, 2)), weights, block_count,
+            jnp.transpose(send_list, (0, 2, 1)), unit_pair, unit_live,
+        )
+        packed = pair_counts(pltpu.with_memory_space_constraint(dealt, pltpu.VMEM))
+        slab, whole = totals(n_gx, n_wa, pltpu.with_memory_space_constraint(packed, pltpu.VMEM))
+        return jnp.transpose(slab * scale, (1, 2, 0)), (whole * (scale / n_gx)).T
 
     return jax.shard_map(
         per_device,

time: 57.5 us -> 52.1 us (0.906); the launches traced: 56.8 us -> 52.6 us
  local copies, waits for them, and re-layouts: 4.25 us -> 0 us
  other arithmetic: 0 us -> 1.21 us
  Pallas kernels: 51.2 us -> 50.1 us
    unnamed x6 -> x0, local copies, waits for them, and re-layouts: 2.16 us -> none
    pallas_call x2 -> x0, local copies, waits for them, and re-layouts: 2.08 us -> none  [totals(): pl.pallas_call(functools.partial(total_kernel, n_gx, n_wa, scale), out_sh...]
    transpose x0 -> x2, other arithmetic: none -> 1.21 us  [per_device(): return (jnp.transpose(slab * scale, (1, 2, 0)), (whole * (scale / n_gx)).T)]
    pallas_call x1, Pallas kernels: 22 us -> 21.3 us  [dealt_blocks(): pl.pallas_call(functools.partial(exchange_kernel, n_gx, n_wa), out_shape=...]
where the time goes in v1:
time: 52.1 us; the launch traced here: 52.6 us
  Pallas kernels  50.1 us (96%)
  between operations  1.3 us (2%)
  other arithmetic  1.21 us (2%)
    pallas_call x1, Pallas kernels, dealt_blocks(): pl.pallas_call(functools.partial(exchange_kernel, n_gx, n_wa), out_shape=...  21.3 us
    pallas_call x1, Pallas kernels, totals(): pl.pallas_call(functools.partial(total_kernel, n_gx, n_wa), out_shape=(pl...  18.6 us
    pallas_call x1, Pallas kernels, pair_counts(): pl.pallas_call(functools.partial(count_kernel, units), out_shape=pltpu.VM...  10.1 us
    transpose x2, other arithmetic, per_device(): return (jnp.transpose(slab * scale, (1, 2, 0)), (whole * (scale / n_gx)).T)  1.21 us

profile of v1, /device:TPU:1, one launch (start us, length us, event | category | flops | bytes accessed | tf_op | source)
XLA Modules:
  0.0 52.6 jit_solution(12957679519608359983)
XLA Ops:
  1.3 21.3 %shard_map.77.blocks_ref = f32[64,8,128]{2,1,0:T(8,128)S(1)} custom-call(s32[16]{0:T(128)} %count_ref.1, s32[1,2,16]{2,1,0:T(2,128)} %bitcast.7, s32[1,32]{1,0:T(1,128)} %pair_ref.1, s32[1]{0:T(128)S(6)} %copy.8.live_ref, f32[3,16,256]{2,1,0:T(8,128)} %bitcast.6, f32[16,256]{1,0:T(8,128)} %wgt_ref.1), custom_call_target="tpu_custom_call" | custom-call | tf_op jit(solution)/shard_map/pallas_call | solution.py:204
  22.6 10.1 %shard_map.78.in_ref = f32[8,128]{1,0:T(8,128)S(1)} custom-call(f32[64,8,128]{2,1,0:T(8,128)S(1)} %shard_map.77.blocks_ref), custom_call_target="tpu_custom_call" | custom-call | tf_op jit(solution)/shard_map/pallas_call | solution.py:385
  32.8 18.6 %shard_map.79 = (f32[20,1,30]{2,1,0:T(1,128)S(1)}, f32[20,30]{1,0:T(8,128)S(1)}) custom-call(f32[8,128]{1,0:T(8,128)S(1)} %shard_map.78.in_ref), custom_call_target="tpu_custom_call" | custom-call | tf_op jit(solution)/shard_map/pallas_call | solution.py:269
  51.4 0.6 %multiply_bitcast_fusion.1 = f32[1,30,20]{1,0,2:T(1,128)} fusion(f32[20,1,30]{2,1,0:T(1,128)S(1)} %get-tuple-element.4), kind=kLoop, calls=%fused_computation.1 | loop fusion | flops 600 | bytes 4800 | tf_op jit(solution)/shard_map/transpose | solution.py:413
  52.0 0.6 %multiply_bitcast_fusion = f32[30,20]{0,1:T(8,128)} fusion(f32[20,30]{1,0:T(8,128)S(1)} %get-tuple-element.5), kind=kLoop, calls=%fused_computation | loop fusion | flops 600 | bytes 4800 | tf_op jit(solution)/shard_map/transpose | solution.py:413
